TPU v7x, 32 devices: a whole 2x2x4 slice. The times are simulated.
32 devices in a mesh: fsdp: 4 (over y, x), seq: 8 (over z, core).
Axes of the slice: x: 2, y: 2, z: 4, core: 2. Of those that a mesh axis runs over, the one named last changes fastest.
Arguments:
- image_input: bfloat16 [4, 1024, 1536], P('fsdp', 'seq'), may hold values from -6 to 6
- text_input: bfloat16 [4, 128, 1536], P('fsdp'), may hold values from -6 to 6
- w_qkv: bfloat16 [1536, 3, 2048], P('fsdp'), may hold values from -0.15625 to 0.15625
- query_gain: float32 [128], replicated, may hold values from 1.2 to 2.4
- key_gain: float32 [128], replicated, may hold values from 1.2 to 2.4
- image_cotangent: bfloat16 [4, 1024, 2048], P('fsdp', 'seq'), may hold values from -6 to 6
- text_cotangent: bfloat16 [4, 128, 2048], P('fsdp'), may hold values from -6 to 6
Outputs:
- image_grad: bfloat16 [4, 1024, 1536], P('fsdp', 'seq')
- text_grad: bfloat16 [4, 128, 1536], P('fsdp')
- weight_grad: float32 [1536, 3, 2048], P('fsdp', None, 'seq')
- gain_grad: float32 [2, 128], replicated
All inputs are finite; a program needn't handle non-finite values.
Results may differ from a plain program's by a relative error of at most 0.018.
The roundings to bfloat16 on the way count: a program that leaves them out, or rounds other values in their place, can miss the bound.
Values may be sent and summed in bfloat16 or wider, within the bound.
A program may use at most 192 MiB of HBM per device.

v0:
```python
import math

import jax
import jax.numpy as jnp
from jax import lax
from jax.sharding import PartitionSpec as P

HEADS = 16
HEAD = 128


epsilon = 1e-06
query_parts = 4


def rms_forward(values, gain):
    floated = values.astype(jnp.float32)
    inverse = lax.rsqrt(jnp.mean(floated * floated, axis=-1, keepdims=True) + epsilon)
    return (floated, inverse, (floated * inverse * gain).astype(jnp.bfloat16))


def rms_backward(floated, inverse, gain, incoming):
    weighted = incoming * gain
    inner_mean = jnp.mean(weighted * floated, axis=-1, keepdims=True)
    grad_input = inverse * weighted - floated * inverse * inverse * inverse * inner_mean
    grad_gain = jnp.sum(incoming * floated * inverse, axis=0)
    return (grad_input, grad_gain)


def head_backward(query_rows, key_rows, value_rows, incoming, query_gain, key_gain):
    query_float, query_inverse, query_normed = rms_forward(query_rows, query_gain)
    key_float, key_inverse, key_normed = rms_forward(key_rows, key_gain)
    length = query_rows.shape[0]
    width = query_rows.shape[1]
    block_rows = length // query_parts
    factor = 1.0 / math.sqrt(width)
    query_blocks = query_normed.reshape(query_parts, block_rows, width)
    incoming_blocks = incoming.reshape(query_parts, block_rows, width)

    def visit(carried, pieces):
        key_total, value_total = carried
        query_piece, incoming_piece = pieces
        scores = jnp.dot(query_piece, key_normed.T, preferred_element_type=jnp.float32) * factor
        attention = jax.nn.softmax(scores, axis=-1)
        attention_grad = jnp.dot(incoming_piece, value_rows.T, preferred_element_type=jnp.float32)
        row_dot = jnp.sum(attention * attention_grad, axis=-1, keepdims=True)
        score_grad = (attention * (attention_grad - row_dot)).astype(jnp.bfloat16)
        value_total = value_total + jnp.dot(
            attention.astype(jnp.bfloat16).T, incoming_piece, preferred_element_type=jnp.float32
        )
        key_total = (
            key_total
            + jnp.dot(score_grad.T, query_piece, preferred_element_type=jnp.float32) * factor
        )
        query_grad = jnp.dot(score_grad, key_normed, preferred_element_type=jnp.float32) * factor
        return ((key_total, value_total), query_grad)

    zeros_init = jnp.zeros((length, width), jnp.float32)
    (key_total, value_total), query_pieces = lax.scan(
        visit, (zeros_init, zeros_init), (query_blocks, incoming_blocks)
    )
    query_grad = query_pieces.reshape(length, width)
    query_input_grad, query_gain_grad = rms_backward(
        query_float, query_inverse, query_gain, query_grad
    )
    key_input_grad, key_gain_grad = rms_backward(key_float, key_inverse, key_gain, key_total)
    stacked = jnp.stack([query_input_grad, key_input_grad, value_total], axis=1).astype(
        jnp.bfloat16
    )
    return (stacked, jnp.stack([query_gain_grad, key_gain_grad], axis=0))


def local(image_input, text_input, w_qkv, query_gain, key_gain, image_cotangent, text_cotangent):
    member_count = lax.axis_size("seq")
    own_index = lax.axis_index("seq")
    local_heads = HEADS // member_count
    own_width = local_heads * HEAD
    offset = own_index * own_width
    text_length = text_input.shape[1]
    image_rows_dev = image_input.shape[1]
    weights = lax.all_gather(w_qkv, "fsdp", axis=0, tiled=True)
    image_triple = jnp.einsum(
        "btd,dch->btch", image_input, weights, preferred_element_type=jnp.float32
    ).astype(jnp.bfloat16)
    stacked = jnp.concatenate([image_triple, image_cotangent[:, :, None, :]], axis=2)
    arrived = lax.all_to_all(stacked, "seq", split_axis=3, concat_axis=1, tiled=True)
    own_weights = lax.dynamic_slice_in_dim(weights, offset, own_width, 2)
    text_triple = jnp.einsum(
        "btd,dch->btch", text_input, own_weights, preferred_element_type=jnp.float32
    ).astype(jnp.bfloat16)
    text_incoming = lax.dynamic_slice_in_dim(text_cotangent, offset, own_width, 2)
    joined_triple = jnp.concatenate([text_triple, arrived[:, :, :3]], axis=1)
    joined_incoming = jnp.concatenate([text_incoming, arrived[:, :, 3]], axis=1)
    batch_rows = joined_triple.shape[0]
    length = joined_triple.shape[1]
    split_triple = joined_triple.reshape(batch_rows, length, 3, local_heads, HEAD)
    split_incoming = joined_incoming.reshape(batch_rows, length, local_heads, HEAD)
    per_head = jax.vmap(head_backward, in_axes=(1, 1, 1, 1, None, None), out_axes=(2, 0))
    per_batch = jax.vmap(per_head, in_axes=(0, 0, 0, 0, None, None), out_axes=(0, 0))
    head_grads, gain_parts = per_batch(
        split_triple[:, :, 0],
        split_triple[:, :, 1],
        split_triple[:, :, 2],
        split_incoming,
        query_gain,
        key_gain,
    )
    head_grads = head_grads.reshape(batch_rows, length, 3, own_width)
    text_grads = head_grads[:, :text_length]
    image_grads = head_grads[:, text_length:]
    gain_total = lax.psum(jnp.sum(gain_parts, axis=(0, 1)), ("fsdp", "seq"))
    image_tokens = lax.all_to_all(image_grads, "seq", split_axis=1, concat_axis=3, tiled=True)
    text_partial = jnp.einsum(
        "btch,dch->btd", text_grads, own_weights, preferred_element_type=jnp.float32
    )
    text_out = lax.psum(text_partial.astype(jnp.bfloat16), "seq")
    image_out = jnp.einsum(
        "btch,dch->btd", image_tokens, weights, preferred_element_type=jnp.float32
    ).astype(jnp.bfloat16)
    text_part = jnp.einsum(
        "btd,btch->dch", text_input, text_grads, preferred_element_type=jnp.float32
    )
    whole_image = lax.all_gather(image_input, "seq", axis=1, tiled=True)

    def add_block(block, running):
        start = (block * image_rows_dev).astype(jnp.int32)
        image_block = lax.dynamic_slice_in_dim(whole_image, start, image_rows_dev, 1)
        grad_block = lax.dynamic_slice_in_dim(image_grads, start, image_rows_dev, 1)
        selected = (block == own_index).astype(jnp.float32)
        term = (
            jnp.einsum("btd,btch->dch", image_block, grad_block, preferred_element_type=jnp.float32)
            + text_part * selected
        )
        rounded = lax.optimization_barrier(term.astype(jnp.bfloat16))
        return running + rounded.astype(jnp.float32)

    start_total = jnp.zeros((image_input.shape[2], 3, own_width), jnp.float32)
    head_total = lax.fori_loop(0, member_count, add_block, start_total)
    grad_weights = lax.psum_scatter(
        head_total.astype(jnp.bfloat16), "fsdp", scatter_dimension=0, tiled=True
    ).astype(jnp.float32)
    return (image_out, text_out, grad_weights, gain_total)


def solution(mesh):
    return jax.shard_map(
        local,
        mesh=mesh,
        in_specs=(
            P("fsdp", "seq", None),
            P("fsdp", None, None),
            P("fsdp", None, None),
            P(),
            P(),
            P("fsdp", "seq", None),
            P("fsdp", None, None),
        ),
        out_specs=(P("fsdp", "seq", None), P("fsdp", None, None), P("fsdp", None, "seq"), P()),
        check_vma=False,
    )
```

profile of v0, /device:TPU:0, one launch (start us, length us, event | category | flops | bytes accessed | tf_op | source)
XLA Modules:
  0.0 548.0 jit_solution(7560957821269184910)
XLA Ops:
  8.1 6.7 %copy.122 = bf16[384,3,2048]{0,2,1:T(8,128)(2,1)} copy(bf16[384,3,2048]{2,0,1:T(8,128)(2,1)} %param.13) | data formatting | bytes 9437184 | tf_op args[2]
  14.8 178.5 %all-gather.3.cloned.1.call-done = bf16[1536,3,2048]{0,2,1:T(8,128)(2,1)} async-done(((bf16[384,3,2048]{0,2,1:T(8,128)(2,1)}), bf16[1536,3,2048]{0,2,1:T(8,128)(2,1)}) %all-gather.3.cloned.1.call-update) | async-done | bytes 18874384 | tf_op jit(solution)/shard_map/all_gather | solution.py:81
  193.3 13.7 %fusion.44 = bf16[1,128,3,2048]{3,1,2,0:T(8,128)(2,1)} fusion(bf16[1536,3,2048]{0,2,1:T(8,128)(2,1)} %all-gather.3.cloned.1.call-done, bf16[1,128,1536]{2,1,0:T(8,128)(2,1)S(1)} %copy-done.16), kind=kOutput, calls=%fused_computation.46 | convolution fusion | flops 2416705536 | bytes 20840448 | tf_op jit(solution)/shard_map/btd,dch->btch/dot_general | solution.py:82
  207.0 1.6 pad_maximum_fusion
  208.6 2.6 copy.124
  211.2 4.6 all-to-all-start
  215.9 2.0 copy.144
  218.3 2.4 fusion.80
  220.7 69.4 %all-to-all-done = bf16[1,128,4,2048]{1,2,0,3:T(4,128)(2,1)S(1)} async-done(((bf16[1,128,4,2048]{1,2,0,3:T(4,128)(2,1)}), bf16[1,128,4,2048]{1,2,0,3:T(4,128)(2,1)S(1)}, u32[]{:S(2)}, u32[]{:S(2)}) %all-to-all-start) | async-done | bytes 2097184 | tf_op jit(solution)/shard_map/all_to_all | solution.py:86
  290.1 1.7 copy.125
  291.8 2.9 copy.126
  296.0 1.7 copy.127
  302.9 52.1 %while.29 = (s32[]{:T(128)}, f32[1,2,1152,128]{3,2,1,0:T(8,128)}, f32[1,2,1152,128]{3,2,1,0:T(8,128)}, f32[4,1,2,288,128]{4,3,0,2,1:T(8,128)}, bf16[4,1,2,288,12...) while((s32[]{:T(128)}, f32[1,2,1152,128]{3,2,1,0:T(8,128)}, ...), condition=%wide.region_6.7_spmd.clone, body=%wide.region_2.6_spmd.clone.sunk | while | flops 858858048 | bytes 69760840 | solution.py:59
  302.9 2.3 fusion.129
  305.1 2.4 multiply_reduce_fusion.2
  307.5 2.2 multiply_convert_fusion.2
  309.8 2.2 fusion.130
  312.1 2.5 fusion.131
  315.9 2.3 fusion.129
  318.1 2.4 multiply_reduce_fusion.2
  320.5 2.2 multiply_convert_fusion.2
  322.8 2.2 fusion.130
  325.1 2.5 fusion.131
  328.9 2.2 fusion.129
  331.2 2.4 multiply_reduce_fusion.2
  333.6 2.2 multiply_convert_fusion.2
  335.8 2.2 fusion.130
  338.1 2.5 fusion.131
  341.9 2.3 fusion.129
  344.2 2.4 multiply_reduce_fusion.2
  346.6 2.2 multiply_convert_fusion.2
  348.9 2.2 fusion.130
  351.2 2.5 fusion.131
  355.0 2.4 copy.138
  357.8 1.7 copy.136
  364.4 2.9 convolution_bitcast_fusion.1
  367.3 6.0 %copy.146 = f32[1536,3,256]{2,0,1:T(8,128)} copy(f32[1536,3,256]{0,2,1:T(8,128)} %convolution_bitcast_fusion.1) | data formatting | bytes 9437184
  373.4 64.9 %while.30 = (s32[]{:T(128)}, f32[1536,3,256]{2,0,1:T(8,128)}, bf16[1,1024,1536]{1,2,0:T(8,128)(2,1)}, bf16[1,1024,3,256]{1,3,2,0:T(8,128)(2,1)}, s32[]{:T(128)},...) while((s32[]{:T(128)}, f32[1536,3,256]{2,0,1:T(8,128)}, ...), condition=%wide.region_11.12_spmd.clone, body=%wide.region_10.11_spmd.clone.sunk | while | flops 309067776 | bytes 19465908 | solution.py:138
  373.4 3.4 add_convert_fusion.2
  376.7 2.7 select_add_fusion.2
  379.4 3.4 add_convert_fusion.2
  382.8 5.0 select_add_fusion.2
  387.8 3.4 add_convert_fusion.2
  391.2 5.0 select_add_fusion.2
  396.3 3.4 add_convert_fusion.2
  399.6 5.0 select_add_fusion.2
  404.7 3.4 add_convert_fusion.2
  408.0 5.0 select_add_fusion.2
  413.1 3.4 add_convert_fusion.2
  416.4 5.0 select_add_fusion.2
  421.5 3.4 add_convert_fusion.2
  424.8 5.0 select_add_fusion.2
  429.9 3.4 add_convert_fusion.2
  433.3 5.0 select_add_fusion.2
  438.3 4.0 convert_element_type.125
  443.7 2.5 copy.140
  446.3 3.6 all-to-all-start.1
  449.9 3.0 fusion.47
  453.0 68.9 %psum.15 = f32[2,128]{1,0:T(2,128)} all-reduce(f32[2,128]{1,0:T(2,128)S(1)} %maximum_reduce_fusion), channel_id=1, replica_groups=mesh['fsdp'=4,'seq'=8] {'fsdp','seq'}, use_global_device_ids=true, to_apply=%region_16.17 | all-reduce | flops 256 | bytes 2048 | tf_op jit(solution)/shard_map/psum | solution.py:111
  521.9 2.3 copy.170
  524.2 2.6 reshape.317
  526.9 9.8 %fusion.48 = bf16[1,128,1536]{2,1,0:T(8,128)(2,1)} fusion(bf16[128,3,2048]{2,0,1:T(8,128)(2,1)S(1)} %reshape.317, bf16[1536,3,2048]{0,2,1:T(8,128)(2,1)} %all-gather.3.cloned.1.call-done), kind=kOutput, calls=%fused_computation.54 | convolution fusion | flops 2416115712 | bytes 20840448 | tf_op jit(solution)/shard_map/btch,dch->btd/dot_general | solution.py:117
  536.6 2.2 convert_element_type.126
  538.8 1.8 copy.191
  (132 shorter events, 18.6 us)
Async XLA Ops:
  8.0 210.1 %copy-start = (bf16[1,128,2048]{2,1,0:T(8,128)(2,1)S(1)}, bf16[1,128,2048]{2,1,0:T(8,128)(2,1)}, u32[]{:S(2)}) copy-start(bf16[1,128,2048]{2,1,0:T(8,128)(2,1)} %param.17) | copy-start | bytes 1572868
  8.0 185.3 %all-gather.3.cloned.1.call-start = ((), (), s32[]{:S(2)}) async-start(), calls=%async_computation.3 | async-start | bytes 23592960 | tf_op jit(solution)/shard_map/all_gather | solution.py:81
  14.7 178.6 %copy-start.16 = (bf16[1,128,1536]{2,1,0:T(8,128)(2,1)S(1)}, bf16[1,128,1536]{2,1,0:T(8,128)(2,1)}, u32[]{:S(2)}) copy-start(bf16[1,128,1536]{2,1,0:T(8,128)(2,1)} %param.11) | copy-start | bytes 1179652
  14.8 192.3 %copy-start.20 = (bf16[1,128,2048]{2,1,0:T(8,128)(2,1)S(1)}, bf16[1,128,2048]{2,1,0:T(8,128)(2,1)}, u32[]{:S(2)}) copy-start(bf16[1,128,2048]{2,1,0:T(8,128)(2,1)} %param.16) | copy-start | bytes 1572868
  211.2 78.9 %all-to-all-start = ((bf16[1,128,4,2048]{1,2,0,3:T(4,128)(2,1)}), bf16[1,128,4,2048]{1,2,0,3:T(4,128)(2,1)S(1)}, u32[]{:S(2)}, u32[]{:S(2)}) async-start(bf16[1,128,4,2048]{1,2,0,3:T(4,128)(2,1)} %copy.124), calls=%async_computation | async-start | bytes 4194304 | tf_op jit(solution)/shard_map/all_to_all | solution.py:86
  215.8 2.5 copy-start.14
  215.8 157.6 %all-gather.5.cloned.1.call-start = ((), (), s32[]{:S(2)}) async-start(), calls=%async_computation.5 | async-start | bytes 3538944 | tf_op jit(solution)/shard_map/all_gather | solution.py:123
  217.9 318.8 %reduce-scatter.2.cloned.1.call-start = ((), (), s32[]{:S(2)}) async-start(), calls=%async_computation.6 | async-start | bytes 2949120 | tf_op jit(solution)/shard_map/reduce_scatter | solution.py:139
  298.0 1.3 copy-start.8
  298.0 1.3 copy-start.10
  298.1 0.9 copy-start.21
  298.1 0.9 copy-start.22
  305.1 2.4 copy-start.2
  307.5 2.3 copy-start.4
  309.8 2.3 copy-start.3
  309.8 2.3 copy-start.17
  312.0 2.6 copy-start.5
  312.1 2.6 copy-start.19
  314.6 1.2 copy-start.18
  318.1 2.4 copy-start.2
  320.5 2.3 copy-start.4
  322.8 2.3 copy-start.3
  322.8 2.3 copy-start.17
  325.1 2.6 copy-start.5
  325.1 2.6 copy-start.19
  327.7 1.2 copy-start.18
  331.2 2.4 copy-start.2
  333.5 2.3 copy-start.4
  335.8 2.3 copy-start.3
  335.8 2.3 copy-start.17
  338.1 2.6 copy-start.5
  338.1 2.6 copy-start.19
  340.7 1.2 copy-start.18
  344.2 2.4 copy-start.2
  346.6 2.3 copy-start.4
  348.8 2.3 copy-start.3
  348.9 2.3 copy-start.17
  351.1 2.6 copy-start.5
  351.2 2.6 copy-start.19
  353.7 1.3 copy-start.18
  355.0 2.4 copy-start.6
  357.8 1.7 copy-start.11
  359.5 1.1 copy-start.9
  361.4 1.1 copy-start.13
  362.7 1.8 copy-start.12
  362.7 1.8 copy-start.15
  442.3 1.4 copy-start.7
  446.3 75.7 %all-to-all-start.1 = ((bf16[1,1024,3,256]{3,2,0,1:T(4,128)(2,1)}), bf16[1,1024,3,256]{3,2,0,1:T(4,128)(2,1)S(1)}, u32[]{:S(2)}, u32[]{:S(2)}) async-start(bf16[1,1024,3,256]{3,2,0,1:T(4,128)(2,1)} %copy.140), calls=%async_computation.1 | async-start | bytes 4194304 | tf_op jit(solution)/shard_map/all_to_all | solution.py:112
  449.9 88.9 %all-reduce.2.cloned.1.call-start = ((), (), s32[]{:S(2)}) async-start(), calls=%async_computation.4 | async-start | bytes 786432 | tf_op jit(solution)/shard_map/psum | solution.py:116
  526.8 13.7 %copy-start.1 = (bf16[1,128,2048]{2,1,0:T(8,128)(2,1)S(1)}, bf16[1,128,2048]{2,1,0:T(8,128)(2,1)}, u32[]{:S(2)}) copy-start(bf16[1,128,2048]{2,1,0:T(8,128)(2,1)} %param.17) | copy-start | bytes 1572868
Sparse Core Ops, SparseCore 0:
  14.9 178.3 all-gather.2
  442.5 35.8 reduce-scatter.1
Sparse Core Ops, SparseCore 1:
  218.5 70.8 all-gather.4
  453.3 69.3 all-reduce.1
where the time goes:
time: 550 us; the launch traced here: 548 us
  waiting for transfers between devices  248 us (45%)
  matrix products  101 us (18%)
  blocking collectives  68.9 us (13%)
  other arithmetic  58.1 us (11%)
  local copies, waits for them, and re-layouts  46.7 us (8%)
  between operations  15.8 us (3%)
  starting transfers between devices  8.54 us (2%)
    all_gather x1, waiting for transfers between devices, local(): weights = lax.all_gather(w_qkv, 'fsdp', axis=0, tiled=True)  179 us
    all_to_all x1, waiting for transfers between devices, local(): lax.all_to_all(stacked, 'seq', split_axis=3, concat_axis=1, tiled=True)  69.4 us
    psum x1, blocking collectives, local(): gain_total = lax.psum(jnp.sum(gain_parts, axis=(0, 1)), ('fsdp', 'seq'))  68.9 us
    add x8, other arithmetic, add_block(): return running + rounded.astype(jnp.float32)  37.9 us
    dot_general x8, matrix products, add_block(): jnp.einsum('btd,btch->dch', image_block, grad_block, preferred_element_ty...  26.9 us
    unnamed x37, local copies, waits for them, and re-layouts  20.7 us
    dot_general x1, matrix products, local(): jnp.einsum('btd,dch->btch', image_input, weights, preferred_element_type=...  13.7 us
  transfers between devices with their start and end apart: 6, of which 2 were waited for; matrix products, arithmetic and copies ran while one was open for 20% of the time, Pallas kernels for 0%

commit v1 on v0

v1 whole, which is shorter than its diff:
```python
import functools
import math

import jax
import jax.numpy as jnp
from jax import lax
from jax.experimental import pallas as pl
from jax.experimental.pallas import tpu as pltpu
from jax.sharding import PartitionSpec as P

EPSILON = 1e-06
MESH = pl.DeviceIdType.MESH
F32 = jnp.float32
BF16 = jnp.bfloat16
NT = (((1,), (1,)), ((), ()))


def kernel(
    nf, ns, image_ref, text_ref, weight_ref, up_ref, text_up_ref, qg_ref, kg_ref,
    image_out, text_out, weight_out, gain_out,
    tokens, weights, ups, triple, grads, qn_s, kn_s, knt_s, dq_s, dk_s, dv_s,
    sib_send, sib_recv, own_part, z_send, z_recv, w_send, w_recv, gain_all, gain_rows, text_half, tokens_t,
    x_send, x_recv, u_send, u_recv, wg_send, wg_recv, sb_send, sb_recv,
    zs_send, zs_recv, ws_send, ws_recv, g_send, g_recv, h_send, h_recv, t_send, t_recv, l_sem,
):
    f = lax.axis_index("fsdp")
    s = lax.axis_index("seq")
    nz = ns // 2
    z = lax.div(s, 2)
    core = lax.rem(s, 2)
    other = 1 - core
    sib = z * 2 + other
    rows = image_ref.shape[0]
    text_rows = text_ref.shape[0]
    parts, w_rows, all_width = weight_ref.shape
    own_width = all_width // ns
    head = qg_ref.shape[1]
    heads = own_width // head
    length = tokens.shape[0]
    piece = text_rows // ns

    def image_at(index, count=1):
        return pl.ds(pl.multiple_of(text_rows + index * rows, rows), count * rows)

    def remote(src, dst, send, recv, target):
        return pltpu.make_async_remote_copy(
            src_ref=src, dst_ref=dst, send_sem=send, recv_sem=recv,
            device_id=target, device_id_type=MESH,
        )

    barrier = pltpu.get_barrier_semaphore()
    for k in range(1, nf):
        pl.semaphore_signal(
            barrier, inc=1, device_id=(lax.rem(f + k, nf), s), device_id_type=MESH
        )
    for k in range(1, ns):
        pl.semaphore_signal(
            barrier, inc=1, device_id=(f, lax.rem(s + k, ns)), device_id_type=MESH
        )
    pl.semaphore_wait(barrier, nf + ns - 2)

    def x_copy(source, target_s, slot):
        return remote(
            image_ref if source is None else tokens.at[image_at(source)],
            tokens.at[image_at(s if source is None else source)],
            x_send.at[slot],
            x_recv.at[s if source is None else source],
            (f, target_s),
        )

    def w_at(index):
        return pl.ds(pl.multiple_of(index * w_rows, w_rows), w_rows)

    def u_at(index):
        return pl.ds(pl.multiple_of(index * own_width, own_width), own_width)

    own_rows = [
        pltpu.make_async_copy(
            weight_ref.at[c, :, u_at(s)],
            weights.at[w_at(f), pl.ds(c * own_width, own_width)],
            l_sem.at[4 + c],
        )
        for c in range(parts)
    ]
    for copy in own_rows:
        copy.start()
    sends = []
    for k in range(1, nz):
        sends.append(x_copy(None, lax.rem(z + k, nz) * 2 + core, k))
    sends.append(x_copy(None, sib, 0))
    for copy in sends:
        copy.start()
    for copy in own_rows:
        copy.wait()
    for k in range(1, nf):
        target = lax.rem(f + k, nf)
        sends.append(
            remote(
                weights.at[w_at(f)], weights.at[w_at(f)], wg_send.at[k], wg_recv.at[f],
                (target, s),
            )
        )
    for k in range(1, ns):
        target = lax.rem(s + k, ns)
        sends.append(
            remote(
                up_ref.at[:, u_at(target)], ups.at[image_at(s)], u_send.at[k], u_recv.at[s],
                (f, target),
            )
        )
    for copy in sends[nz:]:
        copy.start()
    locals_ = [
        pltpu.make_async_copy(image_ref, tokens.at[image_at(s)], l_sem.at[0]),
        pltpu.make_async_copy(text_ref, tokens.at[pl.ds(0, text_rows)], l_sem.at[1]),
        pltpu.make_async_copy(up_ref.at[:, u_at(s)], ups.at[image_at(s)], l_sem.at[2]),
        pltpu.make_async_copy(
            text_up_ref.at[:, u_at(s)], ups.at[pl.ds(0, text_rows)], l_sem.at[3]
        ),
    ]
    for copy in locals_:
        copy.start()
    for copy in locals_:
        copy.wait()
    for k in range(1, nf):
        source = lax.rem(f - k + nf, nf)
        remote(
            weights.at[w_at(f)], weights.at[w_at(source)], wg_send.at[k], wg_recv.at[source], (f, s)
        ).wait_recv()

    def project(at):
        tokens_t[:, at] = tokens[at, :].T
        triple[at, :] = jnp.dot(
            tokens[at, :], weights[...], preferred_element_type=F32
        ).astype(BF16)

    project(pl.ds(0, text_rows))
    forwards = []
    for k in range(nz):
        zt = lax.rem(z - k + nz, nz)
        if k:
            near = zt * 2 + core
            remote(
                image_ref, tokens.at[image_at(near)], x_send.at[k], x_recv.at[near], (f, s)
            ).wait_recv()
            forward = x_copy(near, sib, nz + k)
            forward.start()
            forwards.append(forward)
        far = zt * 2 + other
        remote(
            image_ref, tokens.at[image_at(far)], x_send.at[k], x_recv.at[far], (f, s)
        ).wait_recv()
        project(image_at(zt * 2, 2))
    for k in range(1, ns):
        source = lax.rem(s - k + ns, ns)
        remote(
            up_ref.at[:, u_at(s)], ups.at[image_at(source)], u_send.at[k], u_recv.at[source],
            (f, s),
        ).wait_recv()

    factor = 1.0 / math.sqrt(head)
    query_gain = qg_ref[...]
    key_gain = kg_ref[...]
    block = max(b for b in range(128, 385, 128) if length % b == 0)

    def columns(c, h):
        return pl.ds(c * own_width + h * head, head)

    def inverse_of(values):
        return lax.rsqrt(jnp.mean(values * values, axis=-1, keepdims=True) + EPSILON)

    def rms_backward(values, gain, incoming):
        inverse = inverse_of(values)
        weighted = incoming * gain
        inner = jnp.mean(weighted * values, axis=-1, keepdims=True)
        grad = inverse * weighted - values * (inverse * inverse * inverse * inner)
        return grad, jnp.sum(incoming * values * inverse, axis=0, keepdims=True)

    gain_q = jnp.zeros((1, head), F32)
    gain_k = jnp.zeros((1, head), F32)
    for h in range(heads):
        qf = triple[:, columns(0, h)].astype(F32)
        qn_s[...] = (qf * inverse_of(qf) * query_gain).astype(BF16)
        kf = triple[:, columns(1, h)].astype(F32)
        kn = (kf * inverse_of(kf) * key_gain).astype(BF16)
        kn_s[...] = kn
        knt_s[...] = kn.astype(F32).T.astype(BF16)
        dk_s[...] = jnp.zeros_like(dk_s)
        dv_s[...] = jnp.zeros_like(dv_s)

        def visit(i, carry, h=h):
            at = pl.ds(pl.multiple_of(i * block, block), block)
            queries = qn_s[at, :]
            upstream = ups[at, pl.ds(h * head, head)]
            scores = lax.dot_general(kn_s[...], queries, NT, preferred_element_type=F32)
            p = jnp.exp(scores * factor)
            p = p * (1.0 / jnp.sum(p, axis=0, keepdims=True))
            dp = lax.dot_general(
                triple[:, columns(2, h)], upstream, NT, preferred_element_type=F32
            )
            dot = jnp.sum(p * dp, axis=0, keepdims=True)
            ds = (p * (dp - dot)).astype(BF16)
            dv_s[...] += jnp.dot(p.astype(BF16), upstream, preferred_element_type=F32)
            dk_s[...] += jnp.dot(ds, queries, preferred_element_type=F32)
            dq_s[at, :] = jnp.dot(knt_s[...], ds, preferred_element_type=F32).T * factor
            return carry

        lax.fori_loop(0, length // block, visit, 0)
        dq, part = rms_backward(triple[:, columns(0, h)].astype(F32), query_gain, dq_s[...])
        gain_q += part
        grads[:, columns(0, h)] = dq.astype(BF16)
        dk, part = rms_backward(
            triple[:, columns(1, h)].astype(F32), key_gain, dk_s[...] * factor
        )
        gain_k += part
        grads[:, columns(1, h)] = dk.astype(BF16)
        grads[:, columns(2, h)] = dv_s[...].astype(BF16)

    gain_all[s, 0:1, :] = gain_q
    gain_all[s, 1:2, :] = gain_k
    for k in range(1, ns):
        copy = remote(
            gain_all.at[s], gain_all.at[s], g_send.at[k], g_recv.at[s], (f, lax.rem(s + k, ns))
        )
        copy.start()
        sends.append(copy)

    def text_at(index):
        return pl.ds(pl.multiple_of(index * piece, piece), piece)

    def share(at):
        return lax.dot_general(grads[at, :], weights[...], NT, preferred_element_type=F32)

    text_share = share(pl.ds(0, text_rows)).astype(BF16)
    text_half[...] = text_share
    siblings = []
    for k in range(nz):
        zt = lax.rem(z + k, nz)
        sib_send[k, pl.ds(0, rows), :] = share(image_at(zt * 2 + other)).astype(BF16)
        sib_send[k, pl.ds(rows, piece), :] = text_half[text_at(zt * 2 + other), :]
        copy = remote(
            sib_send.at[k], sib_recv.at[k], sb_send.at[k], sb_recv.at[k], (f, sib)
        )
        copy.start()
        siblings.append(copy)
    crossing = []
    for k in list(range(1, nz)) + [0]:
        zt = lax.rem(z + k, nz)
        mine = share(image_at(zt * 2 + core))
        siblings[k].wait_recv()
        total = mine + sib_recv[k, pl.ds(0, rows), :].astype(F32)
        text_total = text_half[text_at(zt * 2 + core), :].astype(F32) + sib_recv[
            k, pl.ds(rows, piece), :
        ].astype(F32)
        if k:
            z_send[k, pl.ds(0, rows), :] = total.astype(BF16)
            z_send[k, pl.ds(rows, piece), :] = text_total.astype(BF16)
            copy = remote(
                z_send.at[k], z_recv.at[k], zs_send.at[k], zs_recv.at[k], (f, zt * 2 + core)
            )
            copy.start()
            crossing.append(copy)
        else:
            own_part[pl.ds(0, rows), :] = total
            own_part[pl.ds(rows, piece), :] = text_total

    outgoing = []
    for k in list(range(1, nf)) + [0]:
        target = lax.rem(f + k, nf)
        at = pl.ds(pl.multiple_of(target * w_rows, w_rows), w_rows)
        term = jnp.dot(tokens_t[at, :], grads[...], preferred_element_type=F32)
        if k:
            w_send[k] = term.astype(BF16)
            copy = remote(
                w_send.at[k], w_recv.at[k], ws_send.at[k], ws_recv.at[k], (target, s)
            )
            copy.start()
            outgoing.append(copy)
        else:
            rounded = term.astype(BF16).astype(F32)
            for c in range(parts):
                weight_out[c] = rounded[:, c * own_width : (c + 1) * own_width]

    for k in range(1, ns):
        source = lax.rem(s - k + ns, ns)
        remote(
            gain_all.at[source], gain_all.at[source], g_send.at[k], g_recv.at[source], (f, s)
        ).wait_recv()
    gain = gain_all[0]
    for i in range(1, ns):
        gain += gain_all[i]
    gain_rows[f] = gain
    for k in range(1, nf):
        copy = remote(
            gain_rows.at[f], gain_rows.at[f], h_send.at[k], h_recv.at[f], (lax.rem(f + k, nf), s)
        )
        copy.start()
        sends.append(copy)
    for copy in crossing:
        copy.wait_recv()
    total = own_part[...]
    for k in range(1, nz):
        total += z_recv[k].astype(F32)
    image_out[...] = total[:rows].astype(BF16)
    text_out[text_at(s), :] = total[rows:].astype(BF16)
    texts = []
    for k in range(1, ns):
        target = lax.rem(s + k, ns)
        copy = remote(
            text_out.at[text_at(s)], text_out.at[text_at(s)], t_send.at[k], t_recv.at[s],
            (f, target),
        )
        copy.start()
        sends.append(copy)
    for copy in outgoing:
        copy.wait_recv()
    for k in range(1, nf):
        for c in range(parts):
            weight_out[c] += w_recv[k, :, c * own_width : (c + 1) * own_width].astype(F32)
    for k in range(1, nf):
        source = lax.rem(f - k + nf, nf)
        remote(
            gain_rows.at[source], gain_rows.at[source], h_send.at[k], h_recv.at[source], (f, s)
        ).wait_recv()
    gain = gain_rows[0]
    for i in range(1, nf):
        gain += gain_rows[i]
    gain_out[...] = gain
    for k in range(1, ns):
        source = lax.rem(s - k + ns, ns)
        remote(
            text_out.at[text_at(source)], text_out.at[text_at(source)], t_send.at[k],
            t_recv.at[source], (f, s),
        ).wait_recv()
    for copy in sends + forwards + siblings + crossing + outgoing:
        copy.wait_send()


def local(nf, ns, image_input, text_input, w_qkv, query_gain, key_gain, image_up, text_up):
    _, rows, depth = image_input.shape
    text_rows = text_input.shape[1]
    w_rows, three, all_width = w_qkv.shape
    own_width = all_width // ns
    head = query_gain.shape[0]
    length = text_rows + rows * ns
    nz = ns // 2
    width3 = three * own_width
    tall = rows + text_rows // ns
    vmem = pl.BlockSpec(memory_space=pltpu.VMEM)
    hbm = pl.BlockSpec(memory_space=pl.ANY)
    dma = pltpu.SemaphoreType.DMA
    image_grad, text_grad, weight_grad, gain = pl.pallas_call(
        functools.partial(kernel, nf, ns),
        out_shape=(
            jax.ShapeDtypeStruct((rows, depth), BF16),
            jax.ShapeDtypeStruct((text_rows, depth), BF16),
            jax.ShapeDtypeStruct((three, w_rows, own_width), F32),
            jax.ShapeDtypeStruct((8, head), F32),
        ),
        in_specs=[vmem, vmem, hbm, vmem, hbm, vmem, vmem],
        out_specs=(vmem,) * 4,
        scratch_shapes=[
            pltpu.VMEM((length, depth), BF16),
            pltpu.VMEM((depth, width3), BF16),
            pltpu.VMEM((length, own_width), BF16),
            pltpu.VMEM((length, width3), BF16),
            pltpu.VMEM((length, width3), BF16),
            pltpu.VMEM((length, head), BF16),
            pltpu.VMEM((length, head), BF16),
            pltpu.VMEM((head, length), BF16),
            pltpu.VMEM((length, head), F32),
            pltpu.VMEM((length, head), F32),
            pltpu.VMEM((length, head), F32),
            pltpu.VMEM((nz, tall, depth), BF16),
            pltpu.VMEM((nz, tall, depth), BF16),
            pltpu.VMEM((tall, depth), F32),
            pltpu.VMEM((nz, tall, depth), BF16),
            pltpu.VMEM((nz, tall, depth), BF16),
            pltpu.VMEM((nf, w_rows, width3), BF16),
            pltpu.VMEM((nf, w_rows, width3), BF16),
            pltpu.VMEM((ns, 8, head), F32),
            pltpu.VMEM((nf, 8, head), F32),
            pltpu.VMEM((text_rows, depth), BF16),
            pltpu.VMEM((depth, length), BF16),
            dma((2 * nz,)), dma((ns,)),
            dma((ns,)), dma((ns,)),
            dma((nf,)), dma((nf,)),
            dma((nz,)), dma((nz,)),
            dma((nz,)), dma((nz,)),
            dma((nf,)), dma((nf,)),
            dma((ns,)), dma((ns,)),
            dma((nf,)), dma((nf,)),
            dma((ns,)), dma((ns,)),
            dma((4 + three,)),
        ],
        compiler_params=pltpu.CompilerParams(
            collective_id=0, has_side_effects=True, vmem_limit_bytes=60 * 1024 * 1024
        ),
        name="joint_backward",
    )(
        image_input[0], text_input[0], w_qkv.transpose(1, 0, 2), image_up[0], text_up[0],
        query_gain.reshape(1, head), key_gain.reshape(1, head),
    )
    return (
        image_grad[None],
        text_grad[None],
        weight_grad.transpose(1, 0, 2),
        gain[:2],
    )


def solution(mesh):
    return jax.shard_map(
        functools.partial(local, mesh.shape["fsdp"], mesh.shape["seq"]),
        mesh=mesh,
        in_specs=(
            P("fsdp", "seq", None),
            P("fsdp", None, None),
            P("fsdp", None, None),
            P(),
            P(),
            P("fsdp", "seq", None),
            P("fsdp", None, None),
        ),
        out_specs=(P("fsdp", "seq", None), P("fsdp", None, None), P("fsdp", None, "seq"), P()),
        check_vma=False,
    )
```

time: 550 us -> 130 us (0.24)
  waiting for transfers between devices: 248 us -> 0 us
  Pallas kernels: 0 us -> 123 us
  matrix products: 101 us -> 0 us
  blocking collectives: 68.9 us -> 0 us
  other arithmetic: 58.1 us -> 0 us
  local copies, waits for them, and re-layouts: 46.7 us -> 5.88 us
  between operations: 15.8 us -> 0.65 us
  starting transfers between devices: 8.54 us -> 0 us
    all_gather x2 -> x0, waiting for transfers between devices: 179 us -> none  [the longest x1 179 us: local(): weights = lax.all_gather(w_qkv, 'fsdp', axis=0, tiled=True)]
    pallas_call x0 -> x1, Pallas kernels: none -> 123 us  [local(): pl.pallas_call(functools.partial(kernel, nf, ns), out_shape=(jax.ShapeDty...]
    dot_general x29 -> x0, matrix products: 92.2 us -> none  [the longest x8 26.9 us: add_block(): jnp.einsum('btd,btch->dch', image_block, grad_block, preferred_element_ty...]
    all_to_all x2 -> x0, waiting for transfers between devices: 69.4 us -> none  [the longest x1 69.4 us: local(): lax.all_to_all(stacked, 'seq', split_axis=3, concat_axis=1, tiled=True)]
    psum x1 -> x0, blocking collectives: 68.9 us -> none  [local(): gain_total = lax.psum(jnp.sum(gain_parts, axis=(0, 1)), ('fsdp', 'seq'))]
    add x8 -> x0, other arithmetic: 37.9 us -> none  [add_block(): return running + rounded.astype(jnp.float32)]
    unnamed x37 -> x5, local copies, waits for them, and re-layouts: 20.7 us -> 4.55 us
    convert_element_type x7 -> x0, other arithmetic: 15.5 us -> none  [the longest x4 8.99 us: visit(): score_grad = (attention * (attention_grad - row_dot)).astype(jnp.bfloat16)]
  transfers between devices with their start and end apart: 6 -> 0, of which waited for: 2 -> 0; matrix products, arithmetic and copies ran while one was open for 20% -> 0% of each run, Pallas kernels for 0% -> 0%
where the time goes in v1:
time: 130 us; the launch traced here: 129 us
  Pallas kernels  123 us (95%)
  local copies, waits for them, and re-layouts  5.88 us (5%)
    pallas_call x1, Pallas kernels, local(): pl.pallas_call(functools.partial(kernel, nf, ns), out_shape=(jax.ShapeDty...  123 us
    unnamed x5, local copies, waits for them, and re-layouts  4.55 us

profile of v1, /device:TPU:0, one launch (start us, length us, event | category | flops | bytes accessed | tf_op | source)
XLA Modules:
  0.0 129.3 jit_solution(10749864297162176938)
XLA Ops:
  0.6 122.7 %joint_backward.1 = (bf16[128,1536]{1,0:T(8,128)(2,1)}, bf16[128,1536]{1,0:T(8,128)(2,1)}, f32[3,384,256]{2,1,0:T(8,128)}, f32[8,128]{1,0:T(8,128)}) custom-call(bf16[128,1536]{1,0:T(8,128)(2,1)} %bitcast.16, bf16[128,1536]{1,0:T(8,128)(2,1)} %bitcast.17, bf16[3,384,2048]{2,1,0:T(8,128)(2,1)} %bitcast.10, bf16[128,2048]{1,0:T(8,128)(2,1)} %bitcast.12, ...), custom_call_target="tpu_custom_call" | custom-call | tf_op jit(solution)/shard_map/joint_backward/pallas_call | solution.py:352
  123.4 0.0 copy-start
  123.4 1.3 %slice.3 = f32[2,128]{1,0:T(2,128)} slice(f32[8,128]{1,0:T(8,128)} %get-tuple-element.11), slice={[0:2], [0:128]} | slice | bytes 2048 | tf_op jit(solution)/shard_map/slice | solution.py:408
  124.7 1.8 %copy.14 = bf16[1,128,1536]{2,1,0:T(8,128)(2,1)} copy(bf16[1,128,1536]{2,1,0:T(8,128)(2,1)} %bitcast.15) | data formatting | bytes 786432
  126.5 1.8 %copy.15 = bf16[1,128,1536]{2,1,0:T(8,128)(2,1)} copy(bf16[1,128,1536]{2,1,0:T(8,128)(2,1)} %bitcast.14) | data formatting | bytes 786432
  128.3 0.0 copy-done
  128.3 1.0 copy.16
Async XLA Ops:
  123.4 4.9 %copy-start = (f32[3,384,256]{2,1,0:T(8,128)S(1)}, f32[3,384,256]{2,1,0:T(8,128)}, u32[]{:S(2)}) copy-start(f32[3,384,256]{2,1,0:T(8,128)} %get-tuple-element.10) | copy-start | bytes 3538948
